TPU v7x, 512 devices: a whole 4x8x8 slice. The times are simulated.
512 devices in a mesh: row: 16 (over y, core), col: 32 (over z, x).
Axes of the slice: x: 4, y: 8, z: 8, core: 2. Of those that a mesh axis runs over, the one named last changes fastest.
Arguments:
- foreground: int32 [4096, 16384], P('row', 'col'), may hold values 0 or 1
- seed_keys: float32 [4096, 16384], P('row', 'col'), may hold values from 1 to 2
Outputs:
- labels: float32 [4096, 16384], P('row', 'col')
All inputs are finite; a program needn't handle non-finite values. No bound on the sum of `foreground` on one device may be relied on, other than what follows from the above.
Results may differ from a plain program's by a relative error of at most 0.0003.
Values sent between devices are 32-bit elements; how exact they have to be, the bound alone decides.
A program may use at most 64 MiB of HBM per device.

v0:
```python
import jax
import jax.numpy as jnp
from jax import lax
from jax.sharding import PartitionSpec as P

SWEEPS = 48


absent_label = 1e30


def extended(x, sides, width):
    for axis, dim in sides:
        count, length = (lax.axis_size(axis), x.shape[dim])
        up = [(i, (i + 1) % count) for i in range(count - 1)]
        down = [(j, i) for i, j in up]
        last = lax.slice_in_dim(x, length - width, length, axis=dim)
        initial = lax.slice_in_dim(x, 0, width, axis=dim)
        before = lax.ppermute(last, axis, up)
        after = lax.ppermute(initial, axis, down)
        x = jnp.concatenate([before, x, after], axis=dim)
    return x


def sweep_once(padded):
    height = padded.shape[0] - 2
    breadth = padded.shape[1] - 2
    center = padded[1 : 1 + height, 1 : 1 + breadth]
    filled = jnp.where(padded > 0, padded, jnp.full_like(padded, absent_label))
    smallest = filled[1 : 1 + height, 1 : 1 + breadth]
    for offset_row in range(3):
        for offset_col in range(3):
            smallest = jnp.minimum(
                smallest,
                filled[offset_row : offset_row + height, offset_col : offset_col + breadth],
            )
    return jnp.where(center > 0, smallest, jnp.zeros_like(center))


def per_device(foreground, seed_keys):
    current = jnp.where(foreground == 1, seed_keys, jnp.zeros_like(seed_keys))

    def advance_group(sweep_index, present):
        grown = extended(present, (("row", 0), ("col", 1)), 4)
        for repeat in range(4):
            grown = sweep_once(grown)
        return grown

    current = lax.fori_loop(0, SWEEPS // 4, advance_group, current)
    return current


def solution(mesh):
    placed = (P("row", "col"), P("row", "col"))
    return jax.shard_map(
        per_device, mesh=mesh, in_specs=placed, out_specs=P("row", "col"), check_vma=False
    )
```

profile of v0, /device:TPU:281, one launch (start us, length us, event | category | flops | bytes accessed | tf_op | source)
XLA Modules:
  0.0 311.5 jit_solution(17961844285933352203)
XLA Ops:
  1.3 309.4 %while.10 = (s32[]{:T(128)}, f32[256,512]{1,0:T(8,128)S(1)}, s32[]{:T(128)}) while((s32[]{:T(128)}, f32[256,512]{1,0:T(8,128)S(1)}, s32[]{:T(128)}) %tuple.36), condition=%wide.region_1.2_spmd, body=%wide.region_0.1_spmd.sunk | while | flops 7502042 | bytes 27415372 | solution.py:49
  16.3 6.5 %collective-permute-done.3 = f32[264,4]{1,0:T(8,128)S(1)} collective-permute-done((f32[264,4]{1,0:T(8,128)S(1)}, f32[264,4]{1,0:T(8,128)S(1)}, u32[]{:S(2)}, u32[]{:S(2)}) %collective-permute-start.3) | collective-permute-done | bytes 4256 | tf_op jit(solution)/shard_map/while/body/eval_jaxpr/ppermute | solution.py:19
  31.0 4.7 %collective-permute-start.1 = (f32[4,512]{1,0:T(4,128)S(1)}, f32[4,512]{1,0:T(4,128)S(1)}, u32[]{:S(2)}, u32[]{:S(2)}) collective-permute-start(f32[4,512]{1,0:T(4,128)S(1)} %get-tuple-element.60), channel_id=1, source_target_pairs={{0,32},{32,64},{64,96},{96,128},{128,160},{160,192},{192,224},{224... | collective-permute-start | bytes 24584 | tf_op jit(solution)/shard_map/while/body/eval_jaxpr/ppermute | solution.py:19
  44.0 5.2 %collective-permute-done.3 = f32[264,4]{1,0:T(8,128)S(1)} collective-permute-done((f32[264,4]{1,0:T(8,128)S(1)}, f32[264,4]{1,0:T(8,128)S(1)}, u32[]{:S(2)}, u32[]{:S(2)}) %collective-permute-start.3) | collective-permute-done | bytes 4256 | tf_op jit(solution)/shard_map/while/body/eval_jaxpr/ppermute | solution.py:19
  56.8 4.5 %collective-permute-start.1 = (f32[4,512]{1,0:T(4,128)S(1)}, f32[4,512]{1,0:T(4,128)S(1)}, u32[]{:S(2)}, u32[]{:S(2)}) collective-permute-start(f32[4,512]{1,0:T(4,128)S(1)} %get-tuple-element.60), channel_id=1, source_target_pairs={{0,32},{32,64},{64,96},{96,128},{128,160},{160,192},{192,224},{224... | collective-permute-start | bytes 24584 | tf_op jit(solution)/shard_map/while/body/eval_jaxpr/ppermute | solution.py:19
  69.6 5.2 %collective-permute-done.3 = f32[264,4]{1,0:T(8,128)S(1)} collective-permute-done((f32[264,4]{1,0:T(8,128)S(1)}, f32[264,4]{1,0:T(8,128)S(1)}, u32[]{:S(2)}, u32[]{:S(2)}) %collective-permute-start.3) | collective-permute-done | bytes 4256 | tf_op jit(solution)/shard_map/while/body/eval_jaxpr/ppermute | solution.py:19
  82.5 4.4 %collective-permute-start.1 = (f32[4,512]{1,0:T(4,128)S(1)}, f32[4,512]{1,0:T(4,128)S(1)}, u32[]{:S(2)}, u32[]{:S(2)}) collective-permute-start(f32[4,512]{1,0:T(4,128)S(1)} %get-tuple-element.60), channel_id=1, source_target_pairs={{0,32},{32,64},{64,96},{96,128},{128,160},{160,192},{192,224},{224... | collective-permute-start | bytes 24584 | tf_op jit(solution)/shard_map/while/body/eval_jaxpr/ppermute | solution.py:19
  95.1 5.2 %collective-permute-done.3 = f32[264,4]{1,0:T(8,128)S(1)} collective-permute-done((f32[264,4]{1,0:T(8,128)S(1)}, f32[264,4]{1,0:T(8,128)S(1)}, u32[]{:S(2)}, u32[]{:S(2)}) %collective-permute-start.3) | collective-permute-done | bytes 4256 | tf_op jit(solution)/shard_map/while/body/eval_jaxpr/ppermute | solution.py:19
  108.2 4.4 %collective-permute-start.1 = (f32[4,512]{1,0:T(4,128)S(1)}, f32[4,512]{1,0:T(4,128)S(1)}, u32[]{:S(2)}, u32[]{:S(2)}) collective-permute-start(f32[4,512]{1,0:T(4,128)S(1)} %get-tuple-element.60), channel_id=1, source_target_pairs={{0,32},{32,64},{64,96},{96,128},{128,160},{160,192},{192,224},{224... | collective-permute-start | bytes 24584 | tf_op jit(solution)/shard_map/while/body/eval_jaxpr/ppermute | solution.py:19
  120.8 5.2 %collective-permute-done.3 = f32[264,4]{1,0:T(8,128)S(1)} collective-permute-done((f32[264,4]{1,0:T(8,128)S(1)}, f32[264,4]{1,0:T(8,128)S(1)}, u32[]{:S(2)}, u32[]{:S(2)}) %collective-permute-start.3) | collective-permute-done | bytes 4256 | tf_op jit(solution)/shard_map/while/body/eval_jaxpr/ppermute | solution.py:19
  133.8 4.4 %collective-permute-start.1 = (f32[4,512]{1,0:T(4,128)S(1)}, f32[4,512]{1,0:T(4,128)S(1)}, u32[]{:S(2)}, u32[]{:S(2)}) collective-permute-start(f32[4,512]{1,0:T(4,128)S(1)} %get-tuple-element.60), channel_id=1, source_target_pairs={{0,32},{32,64},{64,96},{96,128},{128,160},{160,192},{192,224},{224... | collective-permute-start | bytes 24584 | tf_op jit(solution)/shard_map/while/body/eval_jaxpr/ppermute | solution.py:19
  146.4 5.2 %collective-permute-done.3 = f32[264,4]{1,0:T(8,128)S(1)} collective-permute-done((f32[264,4]{1,0:T(8,128)S(1)}, f32[264,4]{1,0:T(8,128)S(1)}, u32[]{:S(2)}, u32[]{:S(2)}) %collective-permute-start.3) | collective-permute-done | bytes 4256 | tf_op jit(solution)/shard_map/while/body/eval_jaxpr/ppermute | solution.py:19
  159.5 4.4 %collective-permute-start.1 = (f32[4,512]{1,0:T(4,128)S(1)}, f32[4,512]{1,0:T(4,128)S(1)}, u32[]{:S(2)}, u32[]{:S(2)}) collective-permute-start(f32[4,512]{1,0:T(4,128)S(1)} %get-tuple-element.60), channel_id=1, source_target_pairs={{0,32},{32,64},{64,96},{96,128},{128,160},{160,192},{192,224},{224... | collective-permute-start | bytes 24584 | tf_op jit(solution)/shard_map/while/body/eval_jaxpr/ppermute | solution.py:19
  172.0 5.2 %collective-permute-done.3 = f32[264,4]{1,0:T(8,128)S(1)} collective-permute-done((f32[264,4]{1,0:T(8,128)S(1)}, f32[264,4]{1,0:T(8,128)S(1)}, u32[]{:S(2)}, u32[]{:S(2)}) %collective-permute-start.3) | collective-permute-done | bytes 4256 | tf_op jit(solution)/shard_map/while/body/eval_jaxpr/ppermute | solution.py:19
  185.1 4.4 %collective-permute-start.1 = (f32[4,512]{1,0:T(4,128)S(1)}, f32[4,512]{1,0:T(4,128)S(1)}, u32[]{:S(2)}, u32[]{:S(2)}) collective-permute-start(f32[4,512]{1,0:T(4,128)S(1)} %get-tuple-element.60), channel_id=1, source_target_pairs={{0,32},{32,64},{64,96},{96,128},{128,160},{160,192},{192,224},{224... | collective-permute-start | bytes 24584 | tf_op jit(solution)/shard_map/while/body/eval_jaxpr/ppermute | solution.py:19
  197.7 5.2 %collective-permute-done.3 = f32[264,4]{1,0:T(8,128)S(1)} collective-permute-done((f32[264,4]{1,0:T(8,128)S(1)}, f32[264,4]{1,0:T(8,128)S(1)}, u32[]{:S(2)}, u32[]{:S(2)}) %collective-permute-start.3) | collective-permute-done | bytes 4256 | tf_op jit(solution)/shard_map/while/body/eval_jaxpr/ppermute | solution.py:19
  210.7 4.4 %collective-permute-start.1 = (f32[4,512]{1,0:T(4,128)S(1)}, f32[4,512]{1,0:T(4,128)S(1)}, u32[]{:S(2)}, u32[]{:S(2)}) collective-permute-start(f32[4,512]{1,0:T(4,128)S(1)} %get-tuple-element.60), channel_id=1, source_target_pairs={{0,32},{32,64},{64,96},{96,128},{128,160},{160,192},{192,224},{224... | collective-permute-start | bytes 24584 | tf_op jit(solution)/shard_map/while/body/eval_jaxpr/ppermute | solution.py:19
  223.3 5.2 %collective-permute-done.3 = f32[264,4]{1,0:T(8,128)S(1)} collective-permute-done((f32[264,4]{1,0:T(8,128)S(1)}, f32[264,4]{1,0:T(8,128)S(1)}, u32[]{:S(2)}, u32[]{:S(2)}) %collective-permute-start.3) | collective-permute-done | bytes 4256 | tf_op jit(solution)/shard_map/while/body/eval_jaxpr/ppermute | solution.py:19
  236.4 4.4 %collective-permute-start.1 = (f32[4,512]{1,0:T(4,128)S(1)}, f32[4,512]{1,0:T(4,128)S(1)}, u32[]{:S(2)}, u32[]{:S(2)}) collective-permute-start(f32[4,512]{1,0:T(4,128)S(1)} %get-tuple-element.60), channel_id=1, source_target_pairs={{0,32},{32,64},{64,96},{96,128},{128,160},{160,192},{192,224},{224... | collective-permute-start | bytes 24584 | tf_op jit(solution)/shard_map/while/body/eval_jaxpr/ppermute | solution.py:19
  248.9 5.2 %collective-permute-done.3 = f32[264,4]{1,0:T(8,128)S(1)} collective-permute-done((f32[264,4]{1,0:T(8,128)S(1)}, f32[264,4]{1,0:T(8,128)S(1)}, u32[]{:S(2)}, u32[]{:S(2)}) %collective-permute-start.3) | collective-permute-done | bytes 4256 | tf_op jit(solution)/shard_map/while/body/eval_jaxpr/ppermute | solution.py:19
  262.0 4.4 %collective-permute-start.1 = (f32[4,512]{1,0:T(4,128)S(1)}, f32[4,512]{1,0:T(4,128)S(1)}, u32[]{:S(2)}, u32[]{:S(2)}) collective-permute-start(f32[4,512]{1,0:T(4,128)S(1)} %get-tuple-element.60), channel_id=1, source_target_pairs={{0,32},{32,64},{64,96},{96,128},{128,160},{160,192},{192,224},{224... | collective-permute-start | bytes 24584 | tf_op jit(solution)/shard_map/while/body/eval_jaxpr/ppermute | solution.py:19
  274.6 5.2 %collective-permute-done.3 = f32[264,4]{1,0:T(8,128)S(1)} collective-permute-done((f32[264,4]{1,0:T(8,128)S(1)}, f32[264,4]{1,0:T(8,128)S(1)}, u32[]{:S(2)}, u32[]{:S(2)}) %collective-permute-start.3) | collective-permute-done | bytes 4256 | tf_op jit(solution)/shard_map/while/body/eval_jaxpr/ppermute | solution.py:19
  287.6 4.4 %collective-permute-start.1 = (f32[4,512]{1,0:T(4,128)S(1)}, f32[4,512]{1,0:T(4,128)S(1)}, u32[]{:S(2)}, u32[]{:S(2)}) collective-permute-start(f32[4,512]{1,0:T(4,128)S(1)} %get-tuple-element.60), channel_id=1, source_target_pairs={{0,32},{32,64},{64,96},{96,128},{128,160},{160,192},{192,224},{224... | collective-permute-start | bytes 24584 | tf_op jit(solution)/shard_map/while/body/eval_jaxpr/ppermute | solution.py:19
  300.2 5.2 %collective-permute-done.3 = f32[264,4]{1,0:T(8,128)S(1)} collective-permute-done((f32[264,4]{1,0:T(8,128)S(1)}, f32[264,4]{1,0:T(8,128)S(1)}, u32[]{:S(2)}, u32[]{:S(2)}) %collective-permute-start.3) | collective-permute-done | bytes 4256 | tf_op jit(solution)/shard_map/while/body/eval_jaxpr/ppermute | solution.py:19
  (160 shorter events, 197.0 us)
Async XLA Ops:
  12.6 10.2 %collective-permute-start.3 = (f32[264,4]{1,0:T(8,128)S(1)}, f32[264,4]{1,0:T(8,128)S(1)}, u32[]{:S(2)}, u32[]{:S(2)}) collective-permute-start(f32[264,4]{1,0:T(8,128)S(1)} %get-tuple-element.62), channel_id=1, source_target_pairs={{0,1},{1,2},{2,3},{3,4},{4,5},{5,6},{6,7},{7,8},{8,9},{9,10},{10,1... | collective-permute-start | bytes 12680 | tf_op jit(solution)/shard_map/while/body/eval_jaxpr/ppermute | solution.py:19
  28.0 7.7 %collective-permute-start = (f32[4,512]{1,0:T(4,128)S(1)}, f32[4,512]{1,0:T(4,128)S(1)}, u32[]{:S(2)}, u32[]{:S(2)}) collective-permute-start(f32[4,512]{1,0:T(4,128)S(1)} %get-tuple-element.59), channel_id=1, source_target_pairs={{32,0},{64,32},{96,64},{128,96},{160,128},{192,160},{224,192},{256... | collective-permute-start | bytes 24584 | tf_op jit(solution)/shard_map/while/body/eval_jaxpr/ppermute | solution.py:20
  36.6 7.4 %collective-permute-start.2 = (f32[264,4]{1,0:T(8,128)S(1)}, f32[264,4]{1,0:T(8,128)S(1)}, u32[]{:S(2)}, u32[]{:S(2)}) collective-permute-start(f32[264,4]{1,0:T(8,128)S(1)} %get-tuple-element.61), channel_id=1, source_target_pairs={{1,0},{2,1},{3,2},{4,3},{5,4},{6,5},{7,6},{8,7},{9,8},{10,9},{11,1... | collective-permute-start | bytes 12680 | tf_op jit(solution)/shard_map/while/body/eval_jaxpr/ppermute | solution.py:20
  38.5 10.7 %collective-permute-start.3 = (f32[264,4]{1,0:T(8,128)S(1)}, f32[264,4]{1,0:T(8,128)S(1)}, u32[]{:S(2)}, u32[]{:S(2)}) collective-permute-start(f32[264,4]{1,0:T(8,128)S(1)} %get-tuple-element.62), channel_id=1, source_target_pairs={{0,1},{1,2},{2,3},{3,4},{4,5},{5,6},{6,7},{7,8},{8,9},{9,10},{10,1... | collective-permute-start | bytes 12680 | tf_op jit(solution)/shard_map/while/body/eval_jaxpr/ppermute | solution.py:19
  62.2 7.3 %collective-permute-start.2 = (f32[264,4]{1,0:T(8,128)S(1)}, f32[264,4]{1,0:T(8,128)S(1)}, u32[]{:S(2)}, u32[]{:S(2)}) collective-permute-start(f32[264,4]{1,0:T(8,128)S(1)} %get-tuple-element.61), channel_id=1, source_target_pairs={{1,0},{2,1},{3,2},{4,3},{5,4},{6,5},{7,6},{8,7},{9,8},{10,9},{11,1... | collective-permute-start | bytes 12680 | tf_op jit(solution)/shard_map/while/body/eval_jaxpr/ppermute | solution.py:20
  64.1 10.7 %collective-permute-start.3 = (f32[264,4]{1,0:T(8,128)S(1)}, f32[264,4]{1,0:T(8,128)S(1)}, u32[]{:S(2)}, u32[]{:S(2)}) collective-permute-start(f32[264,4]{1,0:T(8,128)S(1)} %get-tuple-element.62), channel_id=1, source_target_pairs={{0,1},{1,2},{2,3},{3,4},{4,5},{5,6},{6,7},{7,8},{8,9},{9,10},{10,1... | collective-permute-start | bytes 12680 | tf_op jit(solution)/shard_map/while/body/eval_jaxpr/ppermute | solution.py:19
  87.9 7.3 %collective-permute-start.2 = (f32[264,4]{1,0:T(8,128)S(1)}, f32[264,4]{1,0:T(8,128)S(1)}, u32[]{:S(2)}, u32[]{:S(2)}) collective-permute-start(f32[264,4]{1,0:T(8,128)S(1)} %get-tuple-element.61), channel_id=1, source_target_pairs={{1,0},{2,1},{3,2},{4,3},{5,4},{6,5},{7,6},{8,7},{9,8},{10,9},{11,1... | collective-permute-start | bytes 12680 | tf_op jit(solution)/shard_map/while/body/eval_jaxpr/ppermute | solution.py:20
  89.8 10.6 %collective-permute-start.3 = (f32[264,4]{1,0:T(8,128)S(1)}, f32[264,4]{1,0:T(8,128)S(1)}, u32[]{:S(2)}, u32[]{:S(2)}) collective-permute-start(f32[264,4]{1,0:T(8,128)S(1)} %get-tuple-element.62), channel_id=1, source_target_pairs={{0,1},{1,2},{2,3},{3,4},{4,5},{5,6},{6,7},{7,8},{8,9},{9,10},{10,1... | collective-permute-start | bytes 12680 | tf_op jit(solution)/shard_map/while/body/eval_jaxpr/ppermute | solution.py:19
  113.5 7.3 %collective-permute-start.2 = (f32[264,4]{1,0:T(8,128)S(1)}, f32[264,4]{1,0:T(8,128)S(1)}, u32[]{:S(2)}, u32[]{:S(2)}) collective-permute-start(f32[264,4]{1,0:T(8,128)S(1)} %get-tuple-element.61), channel_id=1, source_target_pairs={{1,0},{2,1},{3,2},{4,3},{5,4},{6,5},{7,6},{8,7},{9,8},{10,9},{11,1... | collective-permute-start | bytes 12680 | tf_op jit(solution)/shard_map/while/body/eval_jaxpr/ppermute | solution.py:20
  115.4 10.6 %collective-permute-start.3 = (f32[264,4]{1,0:T(8,128)S(1)}, f32[264,4]{1,0:T(8,128)S(1)}, u32[]{:S(2)}, u32[]{:S(2)}) collective-permute-start(f32[264,4]{1,0:T(8,128)S(1)} %get-tuple-element.62), channel_id=1, source_target_pairs={{0,1},{1,2},{2,3},{3,4},{4,5},{5,6},{6,7},{7,8},{8,9},{9,10},{10,1... | collective-permute-start | bytes 12680 | tf_op jit(solution)/shard_map/while/body/eval_jaxpr/ppermute | solution.py:19
  139.1 7.3 %collective-permute-start.2 = (f32[264,4]{1,0:T(8,128)S(1)}, f32[264,4]{1,0:T(8,128)S(1)}, u32[]{:S(2)}, u32[]{:S(2)}) collective-permute-start(f32[264,4]{1,0:T(8,128)S(1)} %get-tuple-element.61), channel_id=1, source_target_pairs={{1,0},{2,1},{3,2},{4,3},{5,4},{6,5},{7,6},{8,7},{9,8},{10,9},{11,1... | collective-permute-start | bytes 12680 | tf_op jit(solution)/shard_map/while/body/eval_jaxpr/ppermute | solution.py:20
  141.1 10.6 %collective-permute-start.3 = (f32[264,4]{1,0:T(8,128)S(1)}, f32[264,4]{1,0:T(8,128)S(1)}, u32[]{:S(2)}, u32[]{:S(2)}) collective-permute-start(f32[264,4]{1,0:T(8,128)S(1)} %get-tuple-element.62), channel_id=1, source_target_pairs={{0,1},{1,2},{2,3},{3,4},{4,5},{5,6},{6,7},{7,8},{8,9},{9,10},{10,1... | collective-permute-start | bytes 12680 | tf_op jit(solution)/shard_map/while/body/eval_jaxpr/ppermute | solution.py:19
  164.8 7.3 %collective-permute-start.2 = (f32[264,4]{1,0:T(8,128)S(1)}, f32[264,4]{1,0:T(8,128)S(1)}, u32[]{:S(2)}, u32[]{:S(2)}) collective-permute-start(f32[264,4]{1,0:T(8,128)S(1)} %get-tuple-element.61), channel_id=1, source_target_pairs={{1,0},{2,1},{3,2},{4,3},{5,4},{6,5},{7,6},{8,7},{9,8},{10,9},{11,1... | collective-permute-start | bytes 12680 | tf_op jit(solution)/shard_map/while/body/eval_jaxpr/ppermute | solution.py:20
  166.7 10.6 %collective-permute-start.3 = (f32[264,4]{1,0:T(8,128)S(1)}, f32[264,4]{1,0:T(8,128)S(1)}, u32[]{:S(2)}, u32[]{:S(2)}) collective-permute-start(f32[264,4]{1,0:T(8,128)S(1)} %get-tuple-element.62), channel_id=1, source_target_pairs={{0,1},{1,2},{2,3},{3,4},{4,5},{5,6},{6,7},{7,8},{8,9},{9,10},{10,1... | collective-permute-start | bytes 12680 | tf_op jit(solution)/shard_map/while/body/eval_jaxpr/ppermute | solution.py:19
  190.4 7.3 %collective-permute-start.2 = (f32[264,4]{1,0:T(8,128)S(1)}, f32[264,4]{1,0:T(8,128)S(1)}, u32[]{:S(2)}, u32[]{:S(2)}) collective-permute-start(f32[264,4]{1,0:T(8,128)S(1)} %get-tuple-element.61), channel_id=1, source_target_pairs={{1,0},{2,1},{3,2},{4,3},{5,4},{6,5},{7,6},{8,7},{9,8},{10,9},{11,1... | collective-permute-start | bytes 12680 | tf_op jit(solution)/shard_map/while/body/eval_jaxpr/ppermute | solution.py:20
  192.3 10.6 %collective-permute-start.3 = (f32[264,4]{1,0:T(8,128)S(1)}, f32[264,4]{1,0:T(8,128)S(1)}, u32[]{:S(2)}, u32[]{:S(2)}) collective-permute-start(f32[264,4]{1,0:T(8,128)S(1)} %get-tuple-element.62), channel_id=1, source_target_pairs={{0,1},{1,2},{2,3},{3,4},{4,5},{5,6},{6,7},{7,8},{8,9},{9,10},{10,1... | collective-permute-start | bytes 12680 | tf_op jit(solution)/shard_map/while/body/eval_jaxpr/ppermute | solution.py:19
  216.1 7.3 %collective-permute-start.2 = (f32[264,4]{1,0:T(8,128)S(1)}, f32[264,4]{1,0:T(8,128)S(1)}, u32[]{:S(2)}, u32[]{:S(2)}) collective-permute-start(f32[264,4]{1,0:T(8,128)S(1)} %get-tuple-element.61), channel_id=1, source_target_pairs={{1,0},{2,1},{3,2},{4,3},{5,4},{6,5},{7,6},{8,7},{9,8},{10,9},{11,1... | collective-permute-start | bytes 12680 | tf_op jit(solution)/shard_map/while/body/eval_jaxpr/ppermute | solution.py:20
  218.0 10.6 %collective-permute-start.3 = (f32[264,4]{1,0:T(8,128)S(1)}, f32[264,4]{1,0:T(8,128)S(1)}, u32[]{:S(2)}, u32[]{:S(2)}) collective-permute-start(f32[264,4]{1,0:T(8,128)S(1)} %get-tuple-element.62), channel_id=1, source_target_pairs={{0,1},{1,2},{2,3},{3,4},{4,5},{5,6},{6,7},{7,8},{8,9},{9,10},{10,1... | collective-permute-start | bytes 12680 | tf_op jit(solution)/shard_map/while/body/eval_jaxpr/ppermute | solution.py:19
  241.7 7.3 %collective-permute-start.2 = (f32[264,4]{1,0:T(8,128)S(1)}, f32[264,4]{1,0:T(8,128)S(1)}, u32[]{:S(2)}, u32[]{:S(2)}) collective-permute-start(f32[264,4]{1,0:T(8,128)S(1)} %get-tuple-element.61), channel_id=1, source_target_pairs={{1,0},{2,1},{3,2},{4,3},{5,4},{6,5},{7,6},{8,7},{9,8},{10,9},{11,1... | collective-permute-start | bytes 12680 | tf_op jit(solution)/shard_map/while/body/eval_jaxpr/ppermute | solution.py:20
  243.6 10.6 %collective-permute-start.3 = (f32[264,4]{1,0:T(8,128)S(1)}, f32[264,4]{1,0:T(8,128)S(1)}, u32[]{:S(2)}, u32[]{:S(2)}) collective-permute-start(f32[264,4]{1,0:T(8,128)S(1)} %get-tuple-element.62), channel_id=1, source_target_pairs={{0,1},{1,2},{2,3},{3,4},{4,5},{5,6},{6,7},{7,8},{8,9},{9,10},{10,1... | collective-permute-start | bytes 12680 | tf_op jit(solution)/shard_map/while/body/eval_jaxpr/ppermute | solution.py:19
  267.3 7.3 %collective-permute-start.2 = (f32[264,4]{1,0:T(8,128)S(1)}, f32[264,4]{1,0:T(8,128)S(1)}, u32[]{:S(2)}, u32[]{:S(2)}) collective-permute-start(f32[264,4]{1,0:T(8,128)S(1)} %get-tuple-element.61), channel_id=1, source_target_pairs={{1,0},{2,1},{3,2},{4,3},{5,4},{6,5},{7,6},{8,7},{9,8},{10,9},{11,1... | collective-permute-start | bytes 12680 | tf_op jit(solution)/shard_map/while/body/eval_jaxpr/ppermute | solution.py:20
  269.3 10.6 %collective-permute-start.3 = (f32[264,4]{1,0:T(8,128)S(1)}, f32[264,4]{1,0:T(8,128)S(1)}, u32[]{:S(2)}, u32[]{:S(2)}) collective-permute-start(f32[264,4]{1,0:T(8,128)S(1)} %get-tuple-element.62), channel_id=1, source_target_pairs={{0,1},{1,2},{2,3},{3,4},{4,5},{5,6},{6,7},{7,8},{8,9},{9,10},{10,1... | collective-permute-start | bytes 12680 | tf_op jit(solution)/shard_map/while/body/eval_jaxpr/ppermute | solution.py:19
  293.0 7.3 %collective-permute-start.2 = (f32[264,4]{1,0:T(8,128)S(1)}, f32[264,4]{1,0:T(8,128)S(1)}, u32[]{:S(2)}, u32[]{:S(2)}) collective-permute-start(f32[264,4]{1,0:T(8,128)S(1)} %get-tuple-element.61), channel_id=1, source_target_pairs={{1,0},{2,1},{3,2},{4,3},{5,4},{6,5},{7,6},{8,7},{9,8},{10,9},{11,1... | collective-permute-start | bytes 12680 | tf_op jit(solution)/shard_map/while/body/eval_jaxpr/ppermute | solution.py:20
  294.9 10.6 %collective-permute-start.3 = (f32[264,4]{1,0:T(8,128)S(1)}, f32[264,4]{1,0:T(8,128)S(1)}, u32[]{:S(2)}, u32[]{:S(2)}) collective-permute-start(f32[264,4]{1,0:T(8,128)S(1)} %get-tuple-element.62), channel_id=1, source_target_pairs={{0,1},{1,2},{2,3},{3,4},{4,5},{5,6},{6,7},{7,8},{8,9},{9,10},{10,1... | collective-permute-start | bytes 12680 | tf_op jit(solution)/shard_map/while/body/eval_jaxpr/ppermute | solution.py:19
  (25 other events, 147.2 us)
where the time goes:
time: 313 us; the launch traced here: 312 us
  starting transfers between devices  148 us (47%)
  waiting for transfers between devices  96.9 us (31%)
  other arithmetic  64.9 us (21%)
    ppermute x24, starting transfers between devices, extended(): before = lax.ppermute(last, axis, up)  92.3 us
    ppermute x24, waiting for transfers between devices, extended(): before = lax.ppermute(last, axis, up)  73.4 us
    ppermute x24, starting transfers between devices, extended(): after = lax.ppermute(initial, axis, down)  55.2 us
    select_n x48, other arithmetic, sweep_once(): filled = jnp.where(padded > 0, padded, jnp.full_like(padded, absent_label))  50.1 us
    ppermute x24, waiting for transfers between devices, extended(): after = lax.ppermute(initial, axis, down)  23.6 us
    select_n x12, other arithmetic, sweep_once(): return jnp.where(center > 0, smallest, jnp.zeros_like(center))  12.3 us
  transfers between devices with their start and end apart: 48, of which 36 were waited for; matrix products, arithmetic and copies ran while one was open for 0% of the time, Pallas kernels for 0%

commit v1 on v0

v1 whole, which is shorter than its diff:
```python
import functools

import jax
import jax.numpy as jnp
from jax import lax
from jax.experimental import pallas as pl
from jax.experimental.pallas import tpu as pltpu
from jax.sharding import PartitionSpec as P

SWEEPS = 48
SCALE = 240.0
SHIFT = 360.0
BIG = 2.0**126
EDGE = 2.0**125
LANES = 128
HALF = 64
ROWS = 256
COLS = 512
WIDE = ROWS + 2 * SWEEPS
BLOCKS = 16
STEPS = WIDE // BLOCKS
LSTEPS = 5
UNROLL = 12
DIRECTIONS = ((-1, -1), (-1, 1), (1, -1), (1, 1), (0, -1), (0, 1), (-1, 0), (1, 0))


def exchange_kernel(fg_hbm, key_hbm, ext, sides, corners, fg, key, packed, load_sem, send_sem, recv_sem):
    row, col = lax.axis_index("row"), lax.axis_index("col")
    rows, cols = lax.axis_size("row"), lax.axis_size("col")
    loads = [
        pltpu.make_async_copy(fg_hbm, fg, load_sem.at[0]),
        pltpu.make_async_copy(key_hbm, key, load_sem.at[1]),
    ]
    for load in loads:
        load.start()

    def present(dr, dc):
        r, c = row + dr, col + dc
        return (r >= 0) & (r < rows) & (c >= 0) & (c < cols)

    barrier = pltpu.get_barrier_semaphore()
    for dr, dc in DIRECTIONS:

        @pl.when(present(dr, dc))
        def _():
            pl.semaphore_signal(
                barrier, inc=1, device_id=(row + dr, col + dc), device_id_type=pl.DeviceIdType.MESH
            )

    for load in loads:
        load.wait()
    ext[:ROWS, :] = jnp.where(fg[...] == 1, jnp.exp2(key[...] * SCALE - SHIFT), BIG)
    low = lax.broadcasted_iota(jnp.int32, (ROWS // 2, LANES), 1) < HALF
    top, bottom = slice(0, ROWS // 2), slice(ROWS // 2, ROWS)
    packed[0] = jnp.where(low, ext[top, :LANES], pltpu.roll(ext[bottom, :LANES], HALF, 1))
    packed[1] = jnp.where(low, pltpu.roll(ext[bottom, COLS - LANES :], HALF, 1), ext[top, COLS - LANES :])

    heights = {-1: pl.ds(0, SWEEPS), 1: pl.ds(ROWS - SWEEPS, SWEEPS)}
    widths = {-1: pl.ds(0, LANES), 1: pl.ds(COLS - LANES, LANES)}
    halos = {-1: pl.ds(ROWS, SWEEPS), 1: pl.ds(ROWS + SWEEPS, SWEEPS)}

    def ends(dr, dc):
        if dr == 0:
            at = 0 if dc < 0 else 1
            return packed.at[at], sides.at[at]
        if dc == 0:
            return ext.at[heights[dr]], ext.at[halos[dr]]
        return ext.at[heights[dr], widths[dc]], corners.at[(1 + dr) + (1 + dc) // 2]

    copies = []
    for i, (dr, dc) in enumerate(DIRECTIONS):
        src, dst = ends(dr, dc)
        copies.append(
            pltpu.make_async_remote_copy(
                src_ref=src,
                dst_ref=dst,
                send_sem=send_sem.at[i],
                recv_sem=recv_sem.at[i],
                device_id=(row + dr, col + dc),
                device_id_type=pl.DeviceIdType.MESH,
            )
        )
    count = jnp.int32(0)
    for dr, dc in DIRECTIONS:
        count += jnp.where(present(dr, dc), 1, 0)
    pl.semaphore_wait(barrier, count)
    for (dr, dc), copy in zip(DIRECTIONS, copies):
        pl.when(present(dr, dc))(copy.start)
    for (dr, dc), copy in zip(DIRECTIONS, copies):

        @pl.when(jnp.logical_not(present(-dr, -dc)))
        def _():
            dst = ends(dr, dc)[1]
            dst[...] = jnp.full(dst.shape, BIG, jnp.float32)

    for (dr, dc), copy in zip(DIRECTIONS, copies):
        pl.when(present(-dr, -dc))(copy.wait_recv)
    for (dr, dc), copy in zip(DIRECTIONS, copies):
        pl.when(present(dr, dc))(copy.wait_send)


def sweep_kernel(ext, sides, corners, out, flat, state, mask, turned):
    lane = lax.broadcasted_iota(jnp.int32, (8, LANES), 1)
    low = lane < HALF
    picks = [(lane * LSTEPS + j) & (LANES - 1) for j in range(LSTEPS)]
    for g in range(WIDE // 8):
        at = slice(8 * g, 8 * g + 8)
        if 8 * g < ROWS // 2:
            side = jnp.where(low, sides[0, at], sides[1, at])
        elif 8 * g < ROWS:
            lower = slice(8 * g - ROWS // 2, 8 * g - ROWS // 2 + 8)
            side = pltpu.roll(jnp.where(low, sides[1, lower], sides[0, lower]), HALF, 1)
        else:
            below = 8 * g < ROWS + SWEEPS
            start = 8 * g - (ROWS if below else ROWS + SWEEPS)
            first = 0 if below else 2
            at_corner = slice(start, start + 8)
            side = jnp.where(low, corners[first, at_corner], corners[first + 1, at_corner])
        sources = [ext[at, LANES * t : LANES * t + LANES] for t in range(4)] + [side]
        for j in range(LSTEPS):
            value = jnp.take_along_axis(sources[0], picks[j], axis=1)
            for t in range(1, LSTEPS):
                first_lane = -(-(LANES * t - j) // LSTEPS)
                value = jnp.where(lane < first_lane, value, jnp.take_along_axis(sources[t], picks[j], axis=1))
            flat[j, at] = value
    big = jnp.full((BLOCKS, LANES), BIG, jnp.bfloat16)
    zero = jnp.zeros((BLOCKS, LANES), jnp.bfloat16)

    def turn(k, first, last):
        turned[k, 0] = pltpu.roll(last, 1, 1)
        turned[k, 1] = pltpu.roll(first, LANES - 1, 1)

    for k in range(STEPS):
        values = [flat[j, pl.ds(k, BLOCKS, stride=STEPS), :].astype(jnp.bfloat16) for j in range(LSTEPS)]
        for j in range(LSTEPS):
            state[k, j] = values[j]
            mask[k, j] = jnp.where(values[j] >= EDGE, big, zero)
        turn(k, values[0], values[-1])

    def across(k):
        a = [state[k, j] for j in range(LSTEPS)]
        p, q = jnp.minimum(a[0], a[1]), jnp.minimum(a[2], a[3])
        return [
            jnp.minimum(turned[k, 0], p),
            jnp.minimum(p, a[2]),
            jnp.minimum(a[1], q),
            jnp.minimum(q, a[4]),
            jnp.minimum(jnp.minimum(a[3], a[4]), turned[k, 1]),
        ]

    def sweeps(i, carry):
        for u in range(UNROLL):
            begin = 2 * u % STEPS
            before = across((begin - 1) % STEPS)
            here = begin_row = across(begin)
            for pair in range(STEPS // 2):
                k = (begin + 2 * pair) % STEPS
                after = across(k + 1)
                follow = begin_row if pair == STEPS // 2 - 1 else across((k + 2) % STEPS)
                above = [pltpu.roll(b, 1, 0) for b in before] if k == 0 else before
                below = [pltpu.roll(f, BLOCKS - 1, 0) for f in follow] if k + 2 == STEPS else follow
                middle = [jnp.minimum(h, a) for h, a in zip(here, after)]
                one = [jnp.maximum(jnp.minimum(a, m), mask[k, j]) for j, (a, m) in enumerate(zip(above, middle))]
                two = [jnp.maximum(jnp.minimum(m, b), mask[k + 1, j]) for j, (m, b) in enumerate(zip(middle, below))]
                for j in range(LSTEPS):
                    state[k, j] = one[j]
                    state[k + 1, j] = two[j]
                turn(k, one[0], one[-1])
                turn(k + 1, two[0], two[-1])
                before, here = after, follow
        return carry

    lax.fori_loop(0, SWEEPS // UNROLL, sweeps, 0)

    for k in range(STEPS):
        for j in range(LSTEPS):
            flat[j, pl.ds(k, BLOCKS, stride=STEPS), :] = state[k, j].astype(jnp.float32)
    for g in range(ROWS // 8):
        at = slice(8 * g, 8 * g + 8)
        values = [flat[j, at] for j in range(LSTEPS)]
        for t in range(4):
            place = lane + LANES * t
            lanes = place // LSTEPS
            step = place - lanes * LSTEPS
            value = jnp.take_along_axis(values[0], lanes, axis=1)
            for j in range(1, LSTEPS):
                value = jnp.where(step == j, jnp.take_along_axis(values[j], lanes, axis=1), value)
            out[at, LANES * t : LANES * t + LANES] = jnp.where(
                value >= EDGE, 0.0, jnp.log2(value) * (1 / SCALE) + SHIFT / SCALE
            )


def per_device(foreground, seed_keys):
    f32 = jnp.float32
    whole = pl.BlockSpec(memory_space=pltpu.VMEM)
    ext, sides, corners = pl.pallas_call(
        exchange_kernel,
        out_shape=[
            jax.ShapeDtypeStruct((WIDE, COLS), f32),
            jax.ShapeDtypeStruct((2, ROWS // 2, LANES), f32),
            jax.ShapeDtypeStruct((4, SWEEPS, LANES), f32),
        ],
        in_specs=[pl.BlockSpec(memory_space=pltpu.HBM)] * 2,
        out_specs=[whole] * 3,
        scratch_shapes=[
            pltpu.VMEM((ROWS, COLS), jnp.int32),
            pltpu.VMEM((ROWS, COLS), f32),
            pltpu.VMEM((2, ROWS // 2, LANES), f32),
            pltpu.SemaphoreType.DMA((2,)),
            pltpu.SemaphoreType.DMA((8,)),
            pltpu.SemaphoreType.DMA((8,)),
        ],
        compiler_params=pltpu.CompilerParams(
            collective_id=0, has_side_effects=True, vmem_limit_bytes=16 * 2**20
        ),
        name="exchange",
    )(foreground, seed_keys)
    bf16 = jnp.bfloat16
    return pl.pallas_call(
        sweep_kernel,
        out_shape=jax.ShapeDtypeStruct((ROWS, COLS), f32),
        in_specs=[whole] * 3,
        out_specs=whole,
        scratch_shapes=[
            pltpu.VMEM((LSTEPS, WIDE, LANES), f32),
            pltpu.VMEM((STEPS, LSTEPS, BLOCKS, LANES), bf16),
            pltpu.VMEM((STEPS, LSTEPS, BLOCKS, LANES), bf16),
            pltpu.VMEM((STEPS, 2, BLOCKS, LANES), bf16),
        ],
        compiler_params=pltpu.CompilerParams(vmem_limit_bytes=16 * 2**20),
        name="sweeps",
    )(ext, sides, corners)


def solution(mesh):
    placed = (P("row", "col"), P("row", "col"))
    return jax.shard_map(
        per_device, mesh=mesh, in_specs=placed, out_specs=P("row", "col"), check_vma=False
    )
```

time: 313 us -> 26.9 us (0.09)
  the two profiles are of different devices: /device:TPU:281 before, /device:TPU:1 now
where the time goes in v1:
time: 26.9 us; the launch traced here: 26.7 us
  Pallas kernels  24.7 us (92%)
  local copies, waits for them, and re-layouts  2.08 us (8%)
    pallas_call x1, Pallas kernels, per_device(): pl.pallas_call(sweep_kernel, out_shape=jax.ShapeDtypeStruct((ROWS, COLS),...  12.9 us
    pallas_call x1, Pallas kernels, per_device(): pl.pallas_call(exchange_kernel, out_shape=[jax.ShapeDtypeStruct((WIDE, CO...  11.7 us
    unnamed x4, local copies, waits for them, and re-layouts  2.08 us

profile of v1, /device:TPU:1, one launch (start us, length us, event | category | flops | bytes accessed | tf_op | source)
XLA Modules:
  0.0 26.7 jit_solution(11975289910727779282)
XLA Ops:
  0.0 0.0 copy-start
  0.0 1.0 %copy-done = s32[256,512]{1,0:T(8,128)S(1)} copy-done((s32[256,512]{1,0:T(8,128)S(1)}, s32[256,512]{1,0:T(8,128)}, u32[]{:S(2)}) %copy-start) | copy-done | bytes 524312
  1.0 0.0 copy-start.1
  1.0 1.0 %copy-done.1 = f32[256,512]{1,0:T(8,128)S(1)} copy-done((f32[256,512]{1,0:T(8,128)S(1)}, f32[256,512]{1,0:T(8,128)}, u32[]{:S(2)}) %copy-start.1) | copy-done | bytes 524312
  2.1 11.7 %exchange.1 = (f32[352,512]{1,0:T(8,128)S(1)}, f32[2,128,128]{2,1,0:T(8,128)S(1)}, f32[4,48,128]{2,1,0:T(8,128)S(1)}) custom-call(s32[256,512]{1,0:T(8,128)S(1)} %copy-done, f32[256,512]{1,0:T(8,128)S(1)} %copy-done.1), custom_call_target="tpu_custom_call" | custom-call | tf_op jit(solution)/shard_map/exchange/pallas_call | solution.py:196
  13.8 12.9 %sweeps.1 = f32[256,512]{1,0:T(8,128)} custom-call(f32[352,512]{1,0:T(8,128)S(1)} %get-tuple-element.8.ext, f32[2,128,128]{2,1,0:T(8,128)S(1)} %get-tuple-element.9.sides, f32[4,48,128]{2,1,0:T(8,128)S(1)} %get-tuple-element.10.corners), custom_call_target="tpu_custom_call" | custom-call | tf_op jit(solution)/shard_map/sweeps/pallas_call | solution.py:219
Async XLA Ops:
  0.0 1.0 %copy-start = (s32[256,512]{1,0:T(8,128)S(1)}, s32[256,512]{1,0:T(8,128)}, u32[]{:S(2)}) copy-start(s32[256,512]{1,0:T(8,128)} %fg_hbm.1) | copy-start | bytes 1572868
  1.0 1.0 %copy-start.1 = (f32[256,512]{1,0:T(8,128)S(1)}, f32[256,512]{1,0:T(8,128)}, u32[]{:S(2)}) copy-start(f32[256,512]{1,0:T(8,128)} %key_hbm.1) | copy-start | bytes 1572868

commit v2 on v1

v2 whole, which is shorter than its diff:
```python
import functools

import jax
import jax.numpy as jnp
from jax import lax
from jax.experimental import pallas as pl
from jax.experimental.pallas import tpu as pltpu
from jax.sharding import PartitionSpec as P

SWEEPS = 48
SCALE = 240.0
SHIFT = 360.0
BIG = 2.0**126
EDGE = 2.0**125
LANES = 128
HALF = 64
ROWS = 256
COLS = 512
WIDE = ROWS + 2 * SWEEPS
BLOCKS = 16
STEPS = WIDE // BLOCKS
LSTEPS = 5
UNROLL = 12
DIRECTIONS = ((-1, -1), (-1, 1), (1, -1), (1, 1), (0, -1), (0, 1), (-1, 0), (1, 0))


def exchange_kernel(fg_hbm, key_hbm, ext, sides, corners, fg, key, packed, load_sem, send_sem, recv_sem):
    row, col = lax.axis_index("row"), lax.axis_index("col")
    rows, cols = lax.axis_size("row"), lax.axis_size("col")
    loads = [
        pltpu.make_async_copy(fg_hbm, fg, load_sem.at[0]),
        pltpu.make_async_copy(key_hbm, key, load_sem.at[1]),
    ]
    for load in loads:
        load.start()

    def present(dr, dc):
        r, c = row + dr, col + dc
        return (r >= 0) & (r < rows) & (c >= 0) & (c < cols)

    barrier = pltpu.get_barrier_semaphore()
    for dr, dc in DIRECTIONS:

        @pl.when(present(dr, dc))
        def _():
            pl.semaphore_signal(
                barrier, inc=1, device_id=(row + dr, col + dc), device_id_type=pl.DeviceIdType.MESH
            )

    for load in loads:
        load.wait()
    for t in range(4):
        at = slice(LANES * t, LANES * t + LANES)
        ext[t, :ROWS] = jnp.where(fg[:, at] == 1, jnp.exp2(key[:, at] * SCALE - SHIFT), BIG)
    low = lax.broadcasted_iota(jnp.int32, (ROWS // 2, LANES), 1) < HALF
    top, bottom = slice(0, ROWS // 2), slice(ROWS // 2, ROWS)
    packed[0] = jnp.where(low, ext[0, top], pltpu.roll(ext[0, bottom], HALF, 1))
    packed[1] = jnp.where(low, pltpu.roll(ext[3, bottom], HALF, 1), ext[3, top])

    heights = {-1: pl.ds(0, SWEEPS), 1: pl.ds(ROWS - SWEEPS, SWEEPS)}
    tiles = {-1: 0, 1: 3}
    halos = {-1: pl.ds(ROWS, SWEEPS), 1: pl.ds(ROWS + SWEEPS, SWEEPS)}

    def ends(dr, dc):
        if dr == 0:
            at = 0 if dc < 0 else 1
            return packed.at[at], sides.at[at]
        if dc == 0:
            return ext.at[:, heights[dr]], ext.at[:, halos[dr]]
        return ext.at[tiles[dc], heights[dr]], corners.at[(1 + dr) + (1 + dc) // 2]

    copies = []
    for i, (dr, dc) in enumerate(DIRECTIONS):
        src, dst = ends(dr, dc)
        copies.append(
            pltpu.make_async_remote_copy(
                src_ref=src,
                dst_ref=dst,
                send_sem=send_sem.at[i],
                recv_sem=recv_sem.at[i],
                device_id=(row + dr, col + dc),
                device_id_type=pl.DeviceIdType.MESH,
            )
        )
    count = jnp.int32(0)
    for dr, dc in DIRECTIONS:
        count += jnp.where(present(dr, dc), 1, 0)
    pl.semaphore_wait(barrier, count)
    for (dr, dc), copy in zip(DIRECTIONS, copies):
        pl.when(present(dr, dc))(copy.start)
    for (dr, dc), copy in zip(DIRECTIONS, copies):

        @pl.when(jnp.logical_not(present(-dr, -dc)))
        def _():
            dst = ends(dr, dc)[1]
            dst[...] = jnp.full(dst.shape, BIG, jnp.float32)

    for (dr, dc), copy in zip(DIRECTIONS, copies):
        pl.when(present(-dr, -dc))(copy.wait_recv)
    for (dr, dc), copy in zip(DIRECTIONS, copies):
        pl.when(present(dr, dc))(copy.wait_send)


def sweep_kernel(ext, sides, corners, out, side, result, sem):
    lane = lax.broadcasted_iota(jnp.int32, (8, LANES), 1)
    low = lane < HALF
    half = ROWS // 2
    for g in range(WIDE // 8):
        start = 8 * g
        if start < half:
            rows = slice(start, start + 8)
            value = jnp.where(low, sides[0, rows], sides[1, rows])
        elif start < ROWS:
            rows = slice(start - half, start - half + 8)
            value = pltpu.roll(jnp.where(low, sides[1, rows], sides[0, rows]), HALF, 1)
        elif start < ROWS + SWEEPS:
            rows = slice(start - ROWS, start - ROWS + 8)
            value = jnp.where(low, corners[0, rows], corners[1, rows])
        else:
            rows = slice(start - ROWS - SWEEPS, start - ROWS - SWEEPS + 8)
            value = jnp.where(low, corners[2, rows], corners[3, rows])
        side[start : start + 8] = value

    bf16, f32 = jnp.bfloat16, jnp.float32
    big = jnp.full((BLOCKS, LANES), BIG, bf16)
    zero = jnp.zeros((BLOCKS, LANES), bf16)
    place = lax.broadcasted_iota(jnp.int32, (BLOCKS, LANES), 1)

    def pick(value, lanes):
        return jnp.take_along_axis(value.astype(f32), lanes, axis=1).astype(bf16)

    def turn(first, last):
        return pltpu.roll(last, 1, 1), pltpu.roll(first, LANES - 1, 1)

    raw = []
    for k in range(STEPS):
        rows = pl.ds(k, BLOCKS, stride=STEPS)
        raw.append([ext[t, rows, :].astype(bf16) for t in range(4)] + [side[rows, :].astype(bf16)])
    state = [[None] * LSTEPS for _ in range(STEPS)]
    for j in range(LSTEPS):
        lanes = (place * LSTEPS + j) & (LANES - 1)
        for k in range(STEPS):
            value = pick(raw[k][0], lanes)
            for t in range(1, LSTEPS):
                value = jnp.where(place < -(-(LANES * t - j) // LSTEPS), value, pick(raw[k][t], lanes))
            state[k][j] = value
    mask = [[jnp.where(v >= EDGE, big, zero) for v in values] for values in state]
    turned = [turn(values[0], values[-1]) for values in state]

    def across(a, t):
        p, q = jnp.minimum(a[0], a[1]), jnp.minimum(a[2], a[3])
        return [
            jnp.minimum(t[0], p),
            jnp.minimum(p, a[2]),
            jnp.minimum(a[1], q),
            jnp.minimum(q, a[4]),
            jnp.minimum(jnp.minimum(a[3], a[4]), t[1]),
        ]

    def sweeps(i, carry):
        state, turned = carry
        state, turned = list(state), list(turned)
        for u in range(UNROLL):
            begin = 2 * u % STEPS
            before = across(state[(begin - 1) % STEPS], turned[(begin - 1) % STEPS])
            here = begin_row = across(state[begin], turned[begin])
            for pair in range(STEPS // 2):
                k = (begin + 2 * pair) % STEPS
                n = (k + 2) % STEPS
                after = across(state[k + 1], turned[k + 1])
                follow = begin_row if pair == STEPS // 2 - 1 else across(state[n], turned[n])
                above = [pltpu.roll(b, 1, 0) for b in before] if k == 0 else before
                below = [pltpu.roll(f, BLOCKS - 1, 0) for f in follow] if k + 2 == STEPS else follow
                middle = [jnp.minimum(h, a) for h, a in zip(here, after)]
                state[k] = [jnp.maximum(jnp.minimum(a, m), c) for a, m, c in zip(above, middle, mask[k])]
                state[k + 1] = [jnp.maximum(jnp.minimum(m, b), c) for m, b, c in zip(middle, below, mask[k + 1])]
                turned[k] = turn(state[k][0], state[k][-1])
                turned[k + 1] = turn(state[k + 1][0], state[k + 1][-1])
                before, here = after, follow
        return state, turned

    state, turned = lax.fori_loop(0, SWEEPS // UNROLL, sweeps, (state, turned))

    stores = []
    for t in range(4):
        at = place + LANES * t
        lanes = at // LSTEPS
        step = at - lanes * LSTEPS
        for k in range(STEPS):
            value = pick(state[k][0], lanes)
            for j in range(1, LSTEPS):
                value = jnp.where(step == j, pick(state[k][j], lanes), value)
            value = value.astype(f32)
            value = jnp.where(value >= EDGE, 0.0, jnp.log2(value) * (1 / SCALE) + SHIFT / SCALE)
            more = (ROWS - 1 - k) // STEPS + 1 - 8
            result[t, pl.ds(k, 8, stride=STEPS), :] = value[:8]
            result[t, pl.ds(k + 8 * STEPS, more, stride=STEPS), :] = value[8 : 8 + more]
        stores.append(pltpu.make_async_copy(result.at[t], out.at[:, pl.ds(LANES * t, LANES)], sem.at[t]))
        stores[-1].start()
    for store in stores:
        store.wait()


def per_device(foreground, seed_keys):
    f32 = jnp.float32
    whole = pl.BlockSpec(memory_space=pltpu.VMEM)
    ext, sides, corners = pl.pallas_call(
        exchange_kernel,
        out_shape=[
            jax.ShapeDtypeStruct((4, WIDE, LANES), f32),
            jax.ShapeDtypeStruct((2, ROWS // 2, LANES), f32),
            jax.ShapeDtypeStruct((4, SWEEPS, LANES), f32),
        ],
        in_specs=[pl.BlockSpec(memory_space=pltpu.HBM)] * 2,
        out_specs=[whole] * 3,
        scratch_shapes=[
            pltpu.VMEM((ROWS, COLS), jnp.int32),
            pltpu.VMEM((ROWS, COLS), f32),
            pltpu.VMEM((2, ROWS // 2, LANES), f32),
            pltpu.SemaphoreType.DMA((2,)),
            pltpu.SemaphoreType.DMA((8,)),
            pltpu.SemaphoreType.DMA((8,)),
        ],
        compiler_params=pltpu.CompilerParams(
            collective_id=0, has_side_effects=True, vmem_limit_bytes=16 * 2**20
        ),
        name="exchange",
    )(pltpu.with_memory_space_constraint(foreground, pltpu.HBM), pltpu.with_memory_space_constraint(seed_keys, pltpu.HBM))
    return pl.pallas_call(
        sweep_kernel,
        out_shape=jax.ShapeDtypeStruct((ROWS, COLS), f32),
        in_specs=[whole] * 3,
        out_specs=pl.BlockSpec(memory_space=pltpu.HBM),
        scratch_shapes=[
            pltpu.VMEM((WIDE, LANES), f32),
            pltpu.VMEM((4, ROWS, LANES), f32),
            pltpu.SemaphoreType.DMA((4,)),
        ],
        compiler_params=pltpu.CompilerParams(vmem_limit_bytes=16 * 2**20),
        name="sweeps",
    )(ext, sides, corners)


def solution(mesh):
    placed = (P("row", "col"), P("row", "col"))
    return jax.shard_map(
        per_device, mesh=mesh, in_specs=placed, out_specs=P("row", "col"), check_vma=False
    )
```

time: 26.9 us -> 18.3 us (0.68)
  Pallas kernels: 24.7 us -> 18.2 us
  local copies, waits for them, and re-layouts: 2.08 us -> 0 us
    pallas_call x1, Pallas kernels: 12.9 us -> 6.49 us  [per_device(): pl.pallas_call(sweep_kernel, out_shape=jax.ShapeDtypeStruct((ROWS, COLS),...]
    unnamed x4 -> x0, local copies, waits for them, and re-layouts: 2.08 us -> none
where the time goes in v2:
time: 18.3 us; the launch traced here: 18.2 us
  Pallas kernels  18.2 us (99%)
    pallas_call x1, Pallas kernels, per_device(): pl.pallas_call(exchange_kernel, out_shape=[jax.ShapeDtypeStruct((4, WIDE,...  11.7 us
    pallas_call x1, Pallas kernels, per_device(): pl.pallas_call(sweep_kernel, out_shape=jax.ShapeDtypeStruct((ROWS, COLS),...  6.49 us

profile of v2, /device:TPU:1, one launch (start us, length us, event | category | flops | bytes accessed | tf_op | source)
XLA Modules:
  0.0 18.2 jit_solution(18357194865052170781)
XLA Ops:
  0.0 11.7 %exchange.1 = (f32[4,352,128]{2,1,0:T(8,128)S(1)}, f32[2,128,128]{2,1,0:T(8,128)S(1)}, f32[4,48,128]{2,1,0:T(8,128)S(1)}) custom-call(s32[256,512]{1,0:T(8,128)} %fg_hbm.1, f32[256,512]{1,0:T(8,128)} %key_hbm.1), custom_call_target="tpu_custom_call" | custom-call | tf_op jit(solution)/shard_map/exchange/pallas_call | solution.py:207
  11.7 6.5 %sweeps.1 = f32[256,512]{1,0:T(8,128)} custom-call(f32[4,352,128]{2,1,0:T(8,128)S(1)} %get-tuple-element.8.ext, f32[2,128,128]{2,1,0:T(8,128)S(1)} %get-tuple-element.9.sides, f32[4,48,128]{2,1,0:T(8,128)S(1)} %get-tuple-element.10.corners), custom_call_target="tpu_custom_call" | custom-call | tf_op jit(solution)/shard_map/sweeps/pallas_call | solution.py:229

commit v3 on v2

v3 whole, which is shorter than its diff:
```python
import jax
import jax.numpy as jnp
from jax import lax
from jax.experimental import pallas as pl
from jax.experimental.pallas import tpu as pltpu
from jax.sharding import PartitionSpec as P

SWEEPS = 48
SCALE = 240.0
SHIFT = 360.0
BIG = 2.0**126
EDGE = 2.0**125
LANES = 128
HALF = 64
ROWS = 256
TILES = 4
WIDE = ROWS + 2 * SWEEPS
PART = SWEEPS // 2
BLOCKS = 16
STEPS = WIDE // BLOCKS
LSTEPS = 5
UNROLL = 24
DIRECTIONS = ((-1, -1), (-1, 1), (1, -1), (1, 1), (0, -1), (0, 1), (-1, 0), (1, 0))


def exchange_kernel(fg_hbm, key_hbm, ext, sides, corners, fg, key, columns, packed, load_sem, send_sem, recv_sem):
    row, col = lax.axis_index("row"), lax.axis_index("col")
    rows, cols = lax.axis_size("row"), lax.axis_size("col")
    loads = {}
    for t in (0, 3, 1, 2):
        tile = pl.ds(LANES * t, LANES)
        loads[t] = (
            pltpu.make_async_copy(fg_hbm.at[:, tile], fg.at[t], load_sem.at[0, t]),
            pltpu.make_async_copy(key_hbm.at[:, tile], key.at[t], load_sem.at[1, t]),
        )
        for load in loads[t]:
            load.start()

    def present(dr, dc):
        r, c = row + dr, col + dc
        return (r >= 0) & (r < rows) & (c >= 0) & (c < cols)

    barrier = pltpu.get_barrier_semaphore()
    count = jnp.int32(0)
    for dr, dc in DIRECTIONS:
        count += jnp.where(present(dr, dc), 1, 0)

        @pl.when(present(dr, dc))
        def _():
            pl.semaphore_signal(
                barrier, inc=1, device_id=(row + dr, col + dc), device_id_type=pl.DeviceIdType.MESH
            )

    heights = {-1: pl.ds(0, SWEEPS), 1: pl.ds(ROWS - SWEEPS, SWEEPS)}
    halos = {-1: pl.ds(ROWS, SWEEPS), 1: pl.ds(ROWS + SWEEPS, SWEEPS)}
    bands = {-1: pl.ds(0, SWEEPS), 1: pl.ds(LANES - SWEEPS, SWEEPS)}

    def corner(dr, dc):
        return (1 + dr) + (1 + dc) // 2

    def ends(dr, dc):
        if dr == 0:
            return columns.at[(1 + dc) // 2], sides.at[bands[dc]]
        if dc == 0:
            return ext.at[:, heights[dr]], ext.at[:, halos[dr]]
        return packed.at[corner(dr, dc)], corners.at[corner(dr, dc)]

    copies = {}
    for i, (dr, dc) in enumerate(DIRECTIONS):
        src, dst = ends(dr, dc)
        copies[dr, dc] = pltpu.make_async_remote_copy(
            src_ref=src,
            dst_ref=dst,
            send_sem=send_sem.at[i],
            recv_sem=recv_sem.at[i],
            device_id=(row + dr, col + dc),
            device_id_type=pl.DeviceIdType.MESH,
        )

    def encode(t):
        for load in loads[t]:
            load.wait()
        ext[t, :ROWS] = jnp.where(fg[t] == 1, jnp.exp2(key[t] * SCALE - SHIFT), BIG)

    low = lax.broadcasted_iota(jnp.int32, (PART, LANES), 1) < HALF
    for t, dc in ((0, -1), (3, 1)):
        encode(t)
        for dr, start in ((-1, 0), (1, ROWS - SWEEPS)):
            first = ext[t, start : start + PART]
            second = pltpu.roll(ext[t, start + PART : start + SWEEPS], HALF, 1)
            packed[corner(dr, dc)] = jnp.where(low, first, second) if dc < 0 else jnp.where(low, second, first)
        turned = ext[t, :ROWS].T
        columns[(1 + dc) // 2] = turned[:SWEEPS] if dc < 0 else turned[LANES - SWEEPS :]

    pl.semaphore_wait(barrier, count)
    for dr, dc in DIRECTIONS[:6]:
        pl.when(present(dr, dc))(copies[dr, dc].start)
    for t in (1, 2):
        encode(t)
    for dr, dc in DIRECTIONS[6:]:
        pl.when(present(dr, dc))(copies[dr, dc].start)

    sides[SWEEPS : LANES - SWEEPS] = jnp.full((LANES - 2 * SWEEPS, ROWS), BIG, jnp.float32)
    for dr, dc in DIRECTIONS:

        @pl.when(jnp.logical_not(present(-dr, -dc)))
        def _():
            dst = ends(dr, dc)[1]
            dst[...] = jnp.full(dst.shape, BIG, jnp.float32)

    for dr, dc in DIRECTIONS:
        pl.when(present(-dr, -dc))(copies[dr, dc].wait_recv)
    for dr, dc in DIRECTIONS:
        pl.when(present(dr, dc))(copies[dr, dc].wait_send)


def sweep_kernel(ext, sides, corners, out, side, result, sem):
    bf16, f32 = jnp.bfloat16, jnp.float32
    side[:ROWS] = sides[...].T
    low = lax.broadcasted_iota(jnp.int32, (PART, LANES), 1) < HALF
    for start, right, left in ((ROWS, 0, 1), (ROWS + SWEEPS, 2, 3)):
        side[start : start + PART] = jnp.where(low, corners[right], corners[left])
        other = jnp.where(low, corners[left], corners[right])
        side[start + PART : start + SWEEPS] = pltpu.roll(other, HALF, 1)

    big = jnp.full((BLOCKS, LANES), BIG, bf16)
    zero = jnp.zeros((BLOCKS, LANES), bf16)
    lane = lax.broadcasted_iota(jnp.int32, (BLOCKS, LANES), 1)
    phase = lane % LSTEPS

    def pick(value, lanes):
        return jnp.take_along_axis(value.astype(f32), lanes, axis=1).astype(bf16)

    def turn(first, last):
        return pltpu.roll(last, 1, 1), pltpu.roll(first, LANES - 1, 1)

    is_phase = [phase == p for p in range(LSTEPS)]
    state = []
    for k in range(STEPS):
        rows = pl.ds(k, BLOCKS, stride=STEPS)
        tiles = [ext[t, rows, :].astype(bf16) for t in range(TILES)] + [side[rows, :].astype(bf16)]
        steps = []
        for j in range(LSTEPS):
            value = tiles[0]
            for t in range(1, LSTEPS):
                value = jnp.where(is_phase[(j - 3 * t) % LSTEPS], tiles[t], value)
            steps.append(pick(value, (lane * LSTEPS + j) & (LANES - 1)))
        state.append(steps)
    mask = [[jnp.where(v >= EDGE, big, zero) for v in values] for values in state]
    turned = [turn(values[0], values[-1]) for values in state]

    def across(a, t):
        p, q = jnp.minimum(a[0], a[1]), jnp.minimum(a[2], a[3])
        return [
            jnp.minimum(t[0], p),
            jnp.minimum(p, a[2]),
            jnp.minimum(a[1], q),
            jnp.minimum(q, a[4]),
            jnp.minimum(jnp.minimum(a[3], a[4]), t[1]),
        ]

    def sweeps(i, carry):
        state, turned = carry
        state, turned = list(state), list(turned)
        for u in range(UNROLL):
            begin = 2 * u % STEPS
            before = across(state[(begin - 1) % STEPS], turned[(begin - 1) % STEPS])
            here = begin_row = across(state[begin], turned[begin])
            for pair in range(STEPS // 2):
                k = (begin + 2 * pair) % STEPS
                n = (k + 2) % STEPS
                after = across(state[k + 1], turned[k + 1])
                follow = begin_row if pair == STEPS // 2 - 1 else across(state[n], turned[n])
                above = [pltpu.roll(b, 1, 0) for b in before] if k == 0 else before
                below = [pltpu.roll(f, BLOCKS - 1, 0) for f in follow] if k + 2 == STEPS else follow
                middle = [jnp.minimum(h, a) for h, a in zip(here, after)]
                state[k] = [jnp.maximum(jnp.minimum(a, m), c) for a, m, c in zip(above, middle, mask[k])]
                state[k + 1] = [jnp.maximum(jnp.minimum(m, b), c) for m, b, c in zip(middle, below, mask[k + 1])]
                turned[k] = turn(state[k][0], state[k][-1])
                turned[k + 1] = turn(state[k + 1][0], state[k + 1][-1])
                before, here = after, follow
        return state, turned

    state, turned = lax.fori_loop(0, SWEEPS // UNROLL, sweeps, (state, turned))

    for k in range(STEPS):
        steps = []
        for j in range(LSTEPS):
            tile = (2 * (j - phase)) % LSTEPS
            steps.append(pick(state[k][j], (LANES * tile + lane) // LSTEPS))
        more = (ROWS - 1 - k) // STEPS + 1 - 8
        for t in range(TILES):
            value = steps[0]
            for j in range(1, LSTEPS):
                value = jnp.where(is_phase[(j - 3 * t) % LSTEPS], steps[j], value)
            value = value.astype(f32)
            value = jnp.where(value >= EDGE, 0.0, jnp.log2(value) * (1 / SCALE) + SHIFT / SCALE)
            result[t, pl.ds(k, 8, stride=STEPS), :] = value[:8]
            result[t, pl.ds(k + 8 * STEPS, more, stride=STEPS), :] = value[8 : 8 + more]
    stores = []
    for t in range(TILES):
        stores.append(pltpu.make_async_copy(result.at[t], out.at[:, pl.ds(LANES * t, LANES)], sem.at[t]))
        stores[-1].start()
    for store in stores:
        store.wait()


def per_device(foreground, seed_keys):
    f32 = jnp.float32
    whole = pl.BlockSpec(memory_space=pltpu.VMEM)
    hbm = pl.BlockSpec(memory_space=pltpu.HBM)
    ext, sides, corners = pl.pallas_call(
        exchange_kernel,
        out_shape=[
            jax.ShapeDtypeStruct((TILES, WIDE, LANES), f32),
            jax.ShapeDtypeStruct((LANES, ROWS), f32),
            jax.ShapeDtypeStruct((4, PART, LANES), f32),
        ],
        in_specs=[hbm] * 2,
        out_specs=[whole] * 3,
        scratch_shapes=[
            pltpu.VMEM((TILES, ROWS, LANES), jnp.int32),
            pltpu.VMEM((TILES, ROWS, LANES), f32),
            pltpu.VMEM((2, SWEEPS, ROWS), f32),
            pltpu.VMEM((4, PART, LANES), f32),
            pltpu.SemaphoreType.DMA((2, TILES)),
            pltpu.SemaphoreType.DMA((8,)),
            pltpu.SemaphoreType.DMA((8,)),
        ],
        compiler_params=pltpu.CompilerParams(
            collective_id=0, has_side_effects=True, vmem_limit_bytes=16 * 2**20
        ),
        name="exchange",
    )(
        pltpu.with_memory_space_constraint(foreground, pltpu.HBM),
        pltpu.with_memory_space_constraint(seed_keys, pltpu.HBM),
    )
    return pl.pallas_call(
        sweep_kernel,
        out_shape=jax.ShapeDtypeStruct((ROWS, TILES * LANES), f32),
        in_specs=[whole] * 3,
        out_specs=hbm,
        scratch_shapes=[
            pltpu.VMEM((WIDE, LANES), f32),
            pltpu.VMEM((TILES, ROWS, LANES), f32),
            pltpu.SemaphoreType.DMA((TILES,)),
        ],
        compiler_params=pltpu.CompilerParams(vmem_limit_bytes=16 * 2**20),
        name="sweeps",
    )(ext, sides, corners)


def solution(mesh):
    placed = (P("row", "col"), P("row", "col"))
    return jax.shard_map(
        per_device, mesh=mesh, in_specs=placed, out_specs=P("row", "col"), check_vma=False
    )
```

time: 18.3 us -> 17 us (0.929)
  Pallas kernels: 18.2 us -> 16.8 us
    pallas_call x2, Pallas kernels: 18.2 us -> 16.8 us  [the longest x1 10.9 us: per_device(): pl.pallas_call(exchange_kernel, out_shape=[jax.ShapeDtypeStruct((TILES, W...]
where the time goes in v3:
time: 17 us; the launch traced here: 16.8 us
  Pallas kernels  16.8 us (99%)
    pallas_call x1, Pallas kernels, per_device(): pl.pallas_call(exchange_kernel, out_shape=[jax.ShapeDtypeStruct((TILES, W...  10.9 us
    pallas_call x1, Pallas kernels, per_device(): pl.pallas_call(sweep_kernel, out_shape=jax.ShapeDtypeStruct((ROWS, TILES...  5.94 us

profile of v3, /device:TPU:1, one launch (start us, length us, event | category | flops | bytes accessed | tf_op | source)
XLA Modules:
  0.0 16.8 jit_solution(14959196406306739911)
XLA Ops:
  0.0 10.9 %exchange.1 = (f32[4,352,128]{2,1,0:T(8,128)S(1)}, f32[128,256]{1,0:T(8,128)S(1)}, f32[4,24,128]{2,1,0:T(8,128)S(1)}) custom-call(s32[256,512]{1,0:T(8,128)} %fg_hbm.1, f32[256,512]{1,0:T(8,128)} %key_hbm.1), custom_call_target="tpu_custom_call" | custom-call | tf_op jit(solution)/shard_map/exchange/pallas_call | solution.py:212
  10.9 5.9 %sweeps.1 = f32[256,512]{1,0:T(8,128)} custom-call(f32[4,352,128]{2,1,0:T(8,128)S(1)} %get-tuple-element.8.ext, f32[128,256]{1,0:T(8,128)S(1)} %get-tuple-element.9.sides, f32[4,24,128]{2,1,0:T(8,128)S(1)} %get-tuple-element.10.corners), custom_call_target="tpu_custom_call" | custom-call | tf_op jit(solution)/shard_map/sweeps/pallas_call | solution.py:238

commit v4 on v3

--- a/solution.py
+++ b/solution.py
@@ -93,8 +93,13 @@
         columns[(1 + dc) // 2] = turned[:SWEEPS] if dc < 0 else turned[LANES - SWEEPS :]
 
     pl.semaphore_wait(barrier, count)
-    for dr, dc in DIRECTIONS[:6]:
+    early = row % 2 == 0
+    for dr, dc in DIRECTIONS[:4]:
+        pl.when(present(dr, dc) & (early if dr > 0 else jnp.logical_not(early)))(copies[dr, dc].start)
+    for dr, dc in DIRECTIONS[4:6]:
         pl.when(present(dr, dc))(copies[dr, dc].start)
+    for dr, dc in DIRECTIONS[:4]:
+        pl.when(present(dr, dc) & (jnp.logical_not(early) if dr > 0 else early))(copies[dr, dc].start)
     for t in (1, 2):
         encode(t)
     for dr, dc in DIRECTIONS[6:]:
@@ -135,19 +140,23 @@
         return pltpu.roll(last, 1, 1), pltpu.roll(first, LANES - 1, 1)
 
     is_phase = [phase == p for p in range(LSTEPS)]
-    state = []
+    tiles = []
     for k in range(STEPS):
         rows = pl.ds(k, BLOCKS, stride=STEPS)
-        tiles = [ext[t, rows, :].astype(bf16) for t in range(TILES)] + [side[rows, :].astype(bf16)]
-        steps = []
-        for j in range(LSTEPS):
-            value = tiles[0]
+        tiles.append([ext[t, rows, :].astype(bf16) for t in range(TILES)] + [side[rows, :].astype(bf16)])
+    state = [[None] * LSTEPS for _ in range(STEPS)]
+    turned = [[None] * 2 for _ in range(STEPS)]
+    for j in (4, 0, 1, 2, 3):
+        for k in range(STEPS):
+            value = tiles[k][0]
             for t in range(1, LSTEPS):
-                value = jnp.where(is_phase[(j - 3 * t) % LSTEPS], tiles[t], value)
-            steps.append(pick(value, (lane * LSTEPS + j) & (LANES - 1)))
-        state.append(steps)
+                value = jnp.where(is_phase[(j - 3 * t) % LSTEPS], tiles[k][t], value)
+            state[k][j] = pick(value, (lane * LSTEPS + j) & (LANES - 1))
+            if j == 4:
+                turned[k][0] = pltpu.roll(state[k][j], 1, 1)
+            if j == 0:
+                turned[k][1] = pltpu.roll(state[k][j], LANES - 1, 1)
     mask = [[jnp.where(v >= EDGE, big, zero) for v in values] for values in state]
-    turned = [turn(values[0], values[-1]) for values in state]
 
     def across(a, t):
         p, q = jnp.minimum(a[0], a[1]), jnp.minimum(a[2], a[3])
@@ -176,29 +185,29 @@
                 middle = [jnp.minimum(h, a) for h, a in zip(here, after)]
                 state[k] = [jnp.maximum(jnp.minimum(a, m), c) for a, m, c in zip(above, middle, mask[k])]
                 state[k + 1] = [jnp.maximum(jnp.minimum(m, b), c) for m, b, c in zip(middle, below, mask[k + 1])]
-                turned[k] = turn(state[k][0], state[k][-1])
-                turned[k + 1] = turn(state[k + 1][0], state[k + 1][-1])
+                turned[k] = list(turn(state[k][0], state[k][-1]))
+                turned[k + 1] = list(turn(state[k + 1][0], state[k + 1][-1]))
                 before, here = after, follow
         return state, turned
 
     state, turned = lax.fori_loop(0, SWEEPS // UNROLL, sweeps, (state, turned))
 
-    for k in range(STEPS):
-        steps = []
-        for j in range(LSTEPS):
-            tile = (2 * (j - phase)) % LSTEPS
-            steps.append(pick(state[k][j], (LANES * tile + lane) // LSTEPS))
-        more = (ROWS - 1 - k) // STEPS + 1 - 8
-        for t in range(TILES):
-            value = steps[0]
+    steps = []
+    for j in range(LSTEPS):
+        tile = (2 * (j - phase)) % LSTEPS
+        lanes = (LANES * tile + lane) // LSTEPS
+        steps.append([pick(state[k][j], lanes) for k in range(STEPS)])
+    stores = []
+    for t in range(TILES):
+        for k in range(STEPS):
+            value = steps[0][k]
             for j in range(1, LSTEPS):
-                value = jnp.where(is_phase[(j - 3 * t) % LSTEPS], steps[j], value)
+                value = jnp.where(is_phase[(j - 3 * t) % LSTEPS], steps[j][k], value)
             value = value.astype(f32)
             value = jnp.where(value >= EDGE, 0.0, jnp.log2(value) * (1 / SCALE) + SHIFT / SCALE)
+            more = (ROWS - 1 - k) // STEPS + 1 - 8
             result[t, pl.ds(k, 8, stride=STEPS), :] = value[:8]
             result[t, pl.ds(k + 8 * STEPS, more, stride=STEPS), :] = value[8 : 8 + more]
-    stores = []
-    for t in range(TILES):
         stores.append(pltpu.make_async_copy(result.at[t], out.at[:, pl.ds(LANES * t, LANES)], sem.at[t]))
         stores[-1].start()
     for store in stores:

time: 17 us -> 16.9 us (level)
  no operation moved by 1% of the time
where the time goes in v4:
time: 16.9 us; the launch traced here: 16.8 us
  Pallas kernels  16.8 us (99%)
    pallas_call x1, Pallas kernels, per_device(): pl.pallas_call(exchange_kernel, out_shape=[jax.ShapeDtypeStruct((TILES, W...  10.9 us
    pallas_call x1, Pallas kernels, per_device(): pl.pallas_call(sweep_kernel, out_shape=jax.ShapeDtypeStruct((ROWS, TILES...  5.88 us

profile of v4, /device:TPU:1, one launch (start us, length us, event | category | flops | bytes accessed | tf_op | source)
XLA Modules:
  0.0 16.8 jit_solution(10806663018920626801)
XLA Ops:
  0.0 10.9 %exchange.1 = (f32[4,352,128]{2,1,0:T(8,128)S(1)}, f32[128,256]{1,0:T(8,128)S(1)}, f32[4,24,128]{2,1,0:T(8,128)S(1)}) custom-call(s32[256,512]{1,0:T(8,128)} %fg_hbm.1, f32[256,512]{1,0:T(8,128)} %key_hbm.1), custom_call_target="tpu_custom_call" | custom-call | tf_op jit(solution)/shard_map/exchange/pallas_call | solution.py:221
  10.9 5.9 %sweeps.1 = f32[256,512]{1,0:T(8,128)} custom-call(f32[4,352,128]{2,1,0:T(8,128)S(1)} %get-tuple-element.8.ext, f32[128,256]{1,0:T(8,128)S(1)} %get-tuple-element.9.sides, f32[4,24,128]{2,1,0:T(8,128)S(1)} %get-tuple-element.10.corners), custom_call_target="tpu_custom_call" | custom-call | tf_op jit(solution)/shard_map/sweeps/pallas_call | solution.py:247

commit v5 on v4

--- a/solution.py
+++ b/solution.py
@@ -19,7 +19,6 @@
 BLOCKS = 16
 STEPS = WIDE // BLOCKS
 LSTEPS = 5
-UNROLL = 24
 DIRECTIONS = ((-1, -1), (-1, 1), (1, -1), (1, 1), (0, -1), (0, 1), (-1, 0), (1, 0))
 
 
@@ -145,17 +144,12 @@
         rows = pl.ds(k, BLOCKS, stride=STEPS)
         tiles.append([ext[t, rows, :].astype(bf16) for t in range(TILES)] + [side[rows, :].astype(bf16)])
     state = [[None] * LSTEPS for _ in range(STEPS)]
-    turned = [[None] * 2 for _ in range(STEPS)]
-    for j in (4, 0, 1, 2, 3):
+    for j in range(LSTEPS):
         for k in range(STEPS):
             value = tiles[k][0]
             for t in range(1, LSTEPS):
                 value = jnp.where(is_phase[(j - 3 * t) % LSTEPS], tiles[k][t], value)
             state[k][j] = pick(value, (lane * LSTEPS + j) & (LANES - 1))
-            if j == 4:
-                turned[k][0] = pltpu.roll(state[k][j], 1, 1)
-            if j == 0:
-                turned[k][1] = pltpu.roll(state[k][j], LANES - 1, 1)
     mask = [[jnp.where(v >= EDGE, big, zero) for v in values] for values in state]
 
     def across(a, t):
@@ -168,46 +162,36 @@
             jnp.minimum(jnp.minimum(a[3], a[4]), t[1]),
         ]
 
-    def sweeps(i, carry):
-        state, turned = carry
-        state, turned = list(state), list(turned)
-        for u in range(UNROLL):
-            begin = 2 * u % STEPS
-            before = across(state[(begin - 1) % STEPS], turned[(begin - 1) % STEPS])
-            here = begin_row = across(state[begin], turned[begin])
-            for pair in range(STEPS // 2):
-                k = (begin + 2 * pair) % STEPS
-                n = (k + 2) % STEPS
-                after = across(state[k + 1], turned[k + 1])
-                follow = begin_row if pair == STEPS // 2 - 1 else across(state[n], turned[n])
-                above = [pltpu.roll(b, 1, 0) for b in before] if k == 0 else before
-                below = [pltpu.roll(f, BLOCKS - 1, 0) for f in follow] if k + 2 == STEPS else follow
-                middle = [jnp.minimum(h, a) for h, a in zip(here, after)]
-                state[k] = [jnp.maximum(jnp.minimum(a, m), c) for a, m, c in zip(above, middle, mask[k])]
-                state[k + 1] = [jnp.maximum(jnp.minimum(m, b), c) for m, b, c in zip(middle, below, mask[k + 1])]
-                turned[k] = list(turn(state[k][0], state[k][-1]))
-                turned[k + 1] = list(turn(state[k + 1][0], state[k + 1][-1]))
-                before, here = after, follow
-        return state, turned
-
-    state, turned = lax.fori_loop(0, SWEEPS // UNROLL, sweeps, (state, turned))
-
-    steps = []
-    for j in range(LSTEPS):
-        tile = (2 * (j - phase)) % LSTEPS
-        lanes = (LANES * tile + lane) // LSTEPS
-        steps.append([pick(state[k][j], lanes) for k in range(STEPS)])
+    turned = [turn(values[0], values[-1]) for values in state]
+    for _ in range(SWEEPS):
+        before = across(state[-1], turned[-1])
+        here = top = across(state[0], turned[0])
+        for k in range(0, STEPS, 2):
+            after = across(state[k + 1], turned[k + 1])
+            follow = across(state[k + 2], turned[k + 2]) if k + 2 < STEPS else top
+            above = before if k else [pltpu.roll(b, 1, 0) for b in before]
+            below = follow if k + 2 < STEPS else [pltpu.roll(f, BLOCKS - 1, 0) for f in follow]
+            middle = [jnp.minimum(h, a) for h, a in zip(here, after)]
+            state[k] = [jnp.maximum(jnp.minimum(a, m), c) for a, m, c in zip(above, middle, mask[k])]
+            state[k + 1] = [jnp.maximum(jnp.minimum(m, b), c) for m, b, c in zip(middle, below, mask[k + 1])]
+            turned[k] = turn(state[k][0], state[k][-1])
+            turned[k + 1] = turn(state[k + 1][0], state[k + 1][-1])
+            before, here = after, follow
+
+    lanes = [(LANES * ((2 * (j - phase)) % LSTEPS) + lane) // LSTEPS for j in range(LSTEPS)]
     stores = []
-    for t in range(TILES):
-        for k in range(STEPS):
-            value = steps[0][k]
+    for k in range(STEPS):
+        steps = [pick(state[k][j], lanes[j]) for j in range(LSTEPS)]
+        more = (ROWS - 1 - k) // STEPS + 1 - 8
+        for t in range(TILES):
+            value = steps[0]
             for j in range(1, LSTEPS):
-                value = jnp.where(is_phase[(j - 3 * t) % LSTEPS], steps[j][k], value)
+                value = jnp.where(is_phase[(j - 3 * t) % LSTEPS], steps[j], value)
             value = value.astype(f32)
             value = jnp.where(value >= EDGE, 0.0, jnp.log2(value) * (1 / SCALE) + SHIFT / SCALE)
-            more = (ROWS - 1 - k) // STEPS + 1 - 8
             result[t, pl.ds(k, 8, stride=STEPS), :] = value[:8]
             result[t, pl.ds(k + 8 * STEPS, more, stride=STEPS), :] = value[8 : 8 + more]
+    for t in range(TILES):
         stores.append(pltpu.make_async_copy(result.at[t], out.at[:, pl.ds(LANES * t, LANES)], sem.at[t]))
         stores[-1].start()
     for store in stores:

time: 16.9 us -> 16.6 us (0.982)
  Pallas kernels: 16.8 us -> 16.4 us
    pallas_call x1, Pallas kernels: 5.88 us -> 5.53 us  [per_device(): pl.pallas_call(sweep_kernel, out_shape=jax.ShapeDtypeStruct((ROWS, TILES...]
where the time goes in v5:
time: 16.6 us; the launch traced here: 16.4 us
  Pallas kernels  16.4 us (99%)
    pallas_call x1, Pallas kernels, per_device(): pl.pallas_call(exchange_kernel, out_shape=[jax.ShapeDtypeStruct((TILES, W...  10.9 us
    pallas_call x1, Pallas kernels, per_device(): pl.pallas_call(sweep_kernel, out_shape=jax.ShapeDtypeStruct((ROWS, TILES...  5.53 us

profile of v5, /device:TPU:1, one launch (start us, length us, event | category | flops | bytes accessed | tf_op | source)
XLA Modules:
  0.0 16.4 jit_solution(9916376742923568963)
XLA Ops:
  0.0 10.9 %exchange.1 = (f32[4,352,128]{2,1,0:T(8,128)S(1)}, f32[128,256]{1,0:T(8,128)S(1)}, f32[4,24,128]{2,1,0:T(8,128)S(1)}) custom-call(s32[256,512]{1,0:T(8,128)} %fg_hbm.1, f32[256,512]{1,0:T(8,128)} %key_hbm.1), custom_call_target="tpu_custom_call" | custom-call | tf_op jit(solution)/shard_map/exchange/pallas_call | solution.py:205
  10.9 5.5 %sweeps.1 = f32[256,512]{1,0:T(8,128)} custom-call(f32[4,352,128]{2,1,0:T(8,128)S(1)} %get-tuple-element.8.ext, f32[128,256]{1,0:T(8,128)S(1)} %get-tuple-element.9.sides, f32[4,24,128]{2,1,0:T(8,128)S(1)} %get-tuple-element.10.corners), custom_call_target="tpu_custom_call" | custom-call | tf_op jit(solution)/shard_map/sweeps/pallas_call | solution.py:231

commit v6 on v5

--- a/solution.py
+++ b/solution.py
@@ -22,7 +22,9 @@
 DIRECTIONS = ((-1, -1), (-1, 1), (1, -1), (1, 1), (0, -1), (0, 1), (-1, 0), (1, 0))
 
 
-def exchange_kernel(fg_hbm, key_hbm, ext, sides, corners, fg, key, columns, packed, load_sem, send_sem, recv_sem):
+def exchange_kernel(
+    fg_hbm, key_hbm, ext, side, sides, corners, fg, key, columns, packed, load_sem, send_sem, recv_sem
+):
     row, col = lax.axis_index("row"), lax.axis_index("col")
     rows, cols = lax.axis_size("row"), lax.axis_size("col")
     loads = {}
@@ -112,21 +114,21 @@
             dst = ends(dr, dc)[1]
             dst[...] = jnp.full(dst.shape, BIG, jnp.float32)
 
-    for dr, dc in DIRECTIONS:
+    for dr, dc in DIRECTIONS[4:6]:
         pl.when(present(-dr, -dc))(copies[dr, dc].wait_recv)
+    side[:ROWS] = sides[...].T
     for dr, dc in DIRECTIONS:
         pl.when(present(dr, dc))(copies[dr, dc].wait_send)
-
-
-def sweep_kernel(ext, sides, corners, out, side, result, sem):
-    bf16, f32 = jnp.bfloat16, jnp.float32
-    side[:ROWS] = sides[...].T
-    low = lax.broadcasted_iota(jnp.int32, (PART, LANES), 1) < HALF
+    for dr, dc in DIRECTIONS[6:] + DIRECTIONS[:4]:
+        pl.when(present(-dr, -dc))(copies[dr, dc].wait_recv)
     for start, right, left in ((ROWS, 0, 1), (ROWS + SWEEPS, 2, 3)):
         side[start : start + PART] = jnp.where(low, corners[right], corners[left])
         other = jnp.where(low, corners[left], corners[right])
         side[start + PART : start + SWEEPS] = pltpu.roll(other, HALF, 1)
 
+
+def sweep_kernel(ext, side, out, result, sem):
+    bf16, f32 = jnp.bfloat16, jnp.float32
     big = jnp.full((BLOCKS, LANES), BIG, bf16)
     zero = jnp.zeros((BLOCKS, LANES), bf16)
     lane = lax.broadcasted_iota(jnp.int32, (BLOCKS, LANES), 1)
@@ -202,16 +204,17 @@
     f32 = jnp.float32
     whole = pl.BlockSpec(memory_space=pltpu.VMEM)
     hbm = pl.BlockSpec(memory_space=pltpu.HBM)
-    ext, sides, corners = pl.pallas_call(
+    ext, side = pl.pallas_call(
         exchange_kernel,
         out_shape=[
             jax.ShapeDtypeStruct((TILES, WIDE, LANES), f32),
-            jax.ShapeDtypeStruct((LANES, ROWS), f32),
-            jax.ShapeDtypeStruct((4, PART, LANES), f32),
+            jax.ShapeDtypeStruct((WIDE, LANES), f32),
         ],
         in_specs=[hbm] * 2,
-        out_specs=[whole] * 3,
+        out_specs=[whole] * 2,
         scratch_shapes=[
+            pltpu.VMEM((LANES, ROWS), f32),
+            pltpu.VMEM((4, PART, LANES), f32),
             pltpu.VMEM((TILES, ROWS, LANES), jnp.int32),
             pltpu.VMEM((TILES, ROWS, LANES), f32),
             pltpu.VMEM((2, SWEEPS, ROWS), f32),
@@ -231,16 +234,15 @@
     return pl.pallas_call(
         sweep_kernel,
         out_shape=jax.ShapeDtypeStruct((ROWS, TILES * LANES), f32),
-        in_specs=[whole] * 3,
+        in_specs=[whole] * 2,
         out_specs=hbm,
         scratch_shapes=[
-            pltpu.VMEM((WIDE, LANES), f32),
             pltpu.VMEM((TILES, ROWS, LANES), f32),
             pltpu.SemaphoreType.DMA((TILES,)),
         ],
         compiler_params=pltpu.CompilerParams(vmem_limit_bytes=16 * 2**20),
         name="sweeps",
-    )(ext, sides, corners)
+    )(ext, side)
 
 
 def solution(mesh):

time: 16.6 us -> 16.5 us (level)
  no operation moved by 1% of the time
where the time goes in v6:
time: 16.5 us; the launch traced here: 16.4 us
  Pallas kernels  16.4 us (99%)
    pallas_call x1, Pallas kernels, per_device(): pl.pallas_call(exchange_kernel, out_shape=[jax.ShapeDtypeStruct((TILES, W...  11 us
    pallas_call x1, Pallas kernels, per_device(): pl.pallas_call(sweep_kernel, out_shape=jax.ShapeDtypeStruct((ROWS, TILES...  5.41 us

profile of v6, /device:TPU:1, one launch (start us, length us, event | category | flops | bytes accessed | tf_op | source)
XLA Modules:
  0.0 16.4 jit_solution(1504058103945443794)
XLA Ops:
  0.0 11.0 %exchange.1 = (f32[4,352,128]{2,1,0:T(8,128)S(1)}, f32[352,128]{1,0:T(8,128)S(1)}) custom-call(s32[256,512]{1,0:T(8,128)} %fg_hbm.1, f32[256,512]{1,0:T(8,128)} %key_hbm.1), custom_call_target="tpu_custom_call" | custom-call | tf_op jit(solution)/shard_map/exchange/pallas_call | solution.py:207
  11.0 5.4 %sweeps.1 = f32[256,512]{1,0:T(8,128)} custom-call(f32[4,352,128]{2,1,0:T(8,128)S(1)} %get-tuple-element.7.ext, f32[352,128]{1,0:T(8,128)S(1)} %get-tuple-element.8.side), custom_call_target="tpu_custom_call" | custom-call | tf_op jit(solution)/shard_map/sweeps/pallas_call | solution.py:234

commit v7 on v6

--- a/solution.py
+++ b/solution.py
@@ -27,6 +27,21 @@
 ):
     row, col = lax.axis_index("row"), lax.axis_index("col")
     rows, cols = lax.axis_size("row"), lax.axis_size("col")
+    def present(dr, dc):
+        r, c = row + dr, col + dc
+        return (r >= 0) & (r < rows) & (c >= 0) & (c < cols)
+
+    barrier = pltpu.get_barrier_semaphore()
+    count = jnp.int32(0)
+    for dr, dc in DIRECTIONS:
+        count += jnp.where(present(dr, dc), 1, 0)
+
+        @pl.when(present(dr, dc))
+        def _():
+            pl.semaphore_signal(
+                barrier, inc=1, device_id=(row + dr, col + dc), device_id_type=pl.DeviceIdType.MESH
+            )
+
     loads = {}
     for t in (0, 3, 1, 2):
         tile = pl.ds(LANES * t, LANES)
@@ -36,21 +51,6 @@
         )
         for load in loads[t]:
             load.start()
-
-    def present(dr, dc):
-        r, c = row + dr, col + dc
-        return (r >= 0) & (r < rows) & (c >= 0) & (c < cols)
-
-    barrier = pltpu.get_barrier_semaphore()
-    count = jnp.int32(0)
-    for dr, dc in DIRECTIONS:
-        count += jnp.where(present(dr, dc), 1, 0)
-
-        @pl.when(present(dr, dc))
-        def _():
-            pl.semaphore_signal(
-                barrier, inc=1, device_id=(row + dr, col + dc), device_id_type=pl.DeviceIdType.MESH
-            )
 
     heights = {-1: pl.ds(0, SWEEPS), 1: pl.ds(ROWS - SWEEPS, SWEEPS)}
     halos = {-1: pl.ds(ROWS, SWEEPS), 1: pl.ds(ROWS + SWEEPS, SWEEPS)}

time: 16.5 us -> 16.5 us (level)
  no operation moved by 1% of the time
where the time goes in v7:
time: 16.5 us; the launch traced here: 16.4 us
  Pallas kernels  16.4 us (99%)
    pallas_call x1, Pallas kernels, per_device(): pl.pallas_call(exchange_kernel, out_shape=[jax.ShapeDtypeStruct((TILES, W...  11 us
    pallas_call x1, Pallas kernels, per_device(): pl.pallas_call(sweep_kernel, out_shape=jax.ShapeDtypeStruct((ROWS, TILES...  5.41 us

profile of v7, /device:TPU:1, one launch (start us, length us, event | category | flops | bytes accessed | tf_op | source)
XLA Modules:
  0.0 16.4 jit_solution(17344627034613924656)
XLA Ops:
  0.0 11.0 %exchange.1 = (f32[4,352,128]{2,1,0:T(8,128)S(1)}, f32[352,128]{1,0:T(8,128)S(1)}) custom-call(s32[256,512]{1,0:T(8,128)} %fg_hbm.1, f32[256,512]{1,0:T(8,128)} %key_hbm.1), custom_call_target="tpu_custom_call" | custom-call | tf_op jit(solution)/shard_map/exchange/pallas_call | solution.py:207
  11.0 5.4 %sweeps.1 = f32[256,512]{1,0:T(8,128)} custom-call(f32[4,352,128]{2,1,0:T(8,128)S(1)} %get-tuple-element.7.ext, f32[352,128]{1,0:T(8,128)S(1)} %get-tuple-element.8.side), custom_call_target="tpu_custom_call" | custom-call | tf_op jit(solution)/shard_map/sweeps/pallas_call | solution.py:234
